TPU v7x, 32 devices: a whole 2x2x4 slice. The times are simulated.
32 devices in a mesh: blk: 16 (over z, x, core), rep: 2 (over y).
Axes of the slice: x: 2, y: 2, z: 4, core: 2. Of those that a mesh axis runs over, the one named last changes fastest.
Arguments:
- measured: float32 [3, 16, 8, 1536], P(None, 'blk', None, 'rep'), may hold values from -4 to 4
- rot_vector: float32 [3, 16, 8, 1536], P(None, 'blk', None, 'rep'), may hold values from -6 to 6
- confidence: float32 [3, 16, 8, 1536], P(None, 'blk', None, 'rep'), may hold values from 0.5 to 2
- first_local: int32 [16, 8, 1536], P('blk', None, 'rep'), may hold values from 0 to 2047
- second_local: int32 [16, 8, 1536], P('blk', None, 'rep'), may hold values from 0 to 2047
- edge_counts: int32 [16, 8, 2], P('blk', None, 'rep'), may hold values from 256 to 768, as said below
- start_angles: float32 [3, 32768], P(None, 'blk'), may hold values from -4 to 4
- anchor: float32 [32768], P('blk'), may hold values from 0.05 to 0.5
Outputs:
- estimate: float32 [3, 32768], P(None, 'blk')
- weights: float32 [16, 8, 1536], P('blk', None, 'rep')
Inputs may be any that keep to these rules, and one draw needn't show every extreme that they name: `edge_counts`: live edges of a tile pair on one device fill its first slots; in every tile some pair holds 768 live edges on one device.
All inputs are finite; a program needn't handle non-finite values.
Results may differ from a plain program's by a relative error of at most 0.0001.
Values sent between devices are 32-bit elements; how exact they have to be, the bound alone decides.
No kernel may reach another device: no remote copies, remote signals or barrier semaphores. Data moves between devices by JAX's collectives and lax.ppermute only.
A program may use at most 128 MiB of HBM per device.

v0:
```python
import jax
import jax.numpy as jnp
from jax import lax
from jax.sharding import PartitionSpec as P

PASSES = 2
ITERS = 2
PAIRS = ((0, 0), (0, 1), (0, 2), (1, 1), (1, 2), (2, 2))
LOOKUP = ((0, 1, 2), (1, 3, 4), (2, 4, 5))
SOFTEN = 0.05


def shifted(value, axis, steps):
    count = lax.axis_size(axis)
    pairs = [(source, (source + steps) % count) for source in range(count)]
    return lax.ppermute(value, axis, pairs)


def rotations(vector):
    squared = vector[0] * vector[0] + vector[1] * vector[1] + vector[2] * vector[2]
    factor = 2.0 / (1.0 + squared)
    zeros = jnp.zeros_like(squared)
    skewed = (
        (zeros, -vector[2], vector[1]),
        (vector[2], zeros, -vector[0]),
        (-vector[1], vector[0], zeros),
    )
    matrix_rows = []
    for first in range(3):
        entries = []
        for second in range(3):
            term = skewed[first][second] + vector[first] * vector[second]
            if first == second:
                entries.append(1.0 + factor * (term - squared))
            else:
                entries.append(factor * term)
        matrix_rows.append(jnp.stack(entries))
    return jnp.stack(matrix_rows)


def rotate(rotation, vector):
    return jnp.sum(rotation * vector[None], axis=1)


def rotate_back(rotation, vector):
    return jnp.sum(rotation * vector[:, None], axis=0)


def block_parts(weighted, rotation):
    far_list = []
    near_list = []
    for first, second in PAIRS:
        near_list.append(jnp.sum(rotation[:, first] * weighted * rotation[:, second], axis=0))
        if first == second:
            far_list.append(weighted[first])
        else:
            far_list.append(jnp.zeros_like(weighted[0]))
    return (jnp.stack(far_list), jnp.stack(near_list))


def inverse_apply(blocks, vector):
    adjugate = jnp.stack(
        [
            blocks[3] * blocks[5] - blocks[4] * blocks[4],
            blocks[2] * blocks[4] - blocks[1] * blocks[5],
            blocks[1] * blocks[4] - blocks[2] * blocks[3],
            blocks[0] * blocks[5] - blocks[2] * blocks[2],
            blocks[1] * blocks[2] - blocks[0] * blocks[4],
            blocks[0] * blocks[3] - blocks[1] * blocks[1],
        ]
    )
    determinant = blocks[0] * adjugate[0] + blocks[1] * adjugate[1] + blocks[2] * adjugate[2]
    result = []
    for first in range(3):
        total = (
            adjugate[LOOKUP[first][0]] * vector[0]
            + adjugate[LOOKUP[first][1]] * vector[1]
            + adjugate[LOOKUP[first][2]] * vector[2]
        )
        result.append(total / determinant)
    return jnp.stack(result)


def spread(terms, index, total):
    return jax.vmap(lambda values: jax.ops.segment_sum(values, index, num_segments=total))(terms)


def on_device(
    measured, rot_vector, confidence, first_local, second_local, edge_counts, start_angles, anchor
):
    tile_cams = start_angles.shape[1]
    pair_count = first_local.shape[1]
    slot_count = first_local.shape[2]
    window_span = pair_count * tile_cams
    first = first_local.reshape(-1)
    second = (
        jnp.arange(pair_count, dtype=jnp.int32)[:, None] * tile_cams + second_local[0]
    ).reshape(-1)
    live = (
        (jnp.arange(slot_count, dtype=jnp.int32)[None, :] < edge_counts[0])
        .astype(jnp.float32)
        .reshape(-1)
    )
    measured = measured.reshape(3, -1)
    confidence = confidence.reshape(3, -1)
    rotation = rotations(rot_vector.reshape(3, -1))
    diagonal = jnp.stack(
        [anchor if first_c == second_c else jnp.zeros_like(anchor) for first_c, second_c in PAIRS]
    )

    def window_of(field):
        window = field
        width = 1
        while width < pair_count:
            ahead = shifted(window, "blk", -width)
            window = jnp.concatenate([window, ahead], axis=1)
            width = width * 2
        return window

    def returned(far_sums):
        current = far_sums
        width = pair_count
        while width > 1:
            half_width = width // 2
            moved = shifted(current[:, half_width:width], "blk", half_width)
            current = current[:, :half_width] + moved
            width = half_width
        return current[:, 0]

    def reduce_halves(sums):
        return lax.psum(sums, "rep")

    def collect(far_terms, near_terms):
        channels = far_terms.shape[0]
        far_sums = spread(far_terms, second, window_span).reshape(channels, pair_count, tile_cams)
        near_sums = spread(near_terms, first, tile_cams)
        return reduce_halves(returned(far_sums) + near_sums)

    def precond_sum(residual, scaled):
        return lax.psum(jnp.sum(residual * scaled), "blk")

    estimate = start_angles
    weights = live
    for sweep_index in range(PASSES):
        window = window_of(estimate)
        misfit = measured - (window[:, second] - rotate(rotation, estimate[:, first]))
        weights = live / jnp.sqrt(jnp.sum(confidence * misfit * misfit, axis=0) + SOFTEN * SOFTEN)
        weighted = weights * confidence
        terms = weighted * misfit
        far_part, near_part = block_parts(weighted, rotation)
        near_terms = jnp.concatenate([-rotate_back(rotation, terms), near_part], axis=0)
        far_terms = jnp.concatenate([terms, far_part], axis=0)
        totals = collect(far_terms, near_terms)
        residual = totals[:3] - anchor * estimate
        blocks = totals[3:] + diagonal
        scaled = inverse_apply(blocks, residual)
        direction = scaled
        norm_now = precond_sum(residual, scaled)
        for inner_index in range(ITERS):
            window = window_of(direction)
            changed = window[:, second] - rotate(rotation, direction[:, first])
            pushed = weighted * changed
            image = collect(pushed, -rotate_back(rotation, pushed)) + anchor * direction
            step_size = norm_now / lax.psum(jnp.sum(direction * image), "blk")
            estimate = estimate + step_size * direction
            residual = residual - step_size * image
            if inner_index + 1 < ITERS:
                scaled = inverse_apply(blocks, residual)
                norm_next = precond_sum(residual, scaled)
                direction = scaled + norm_next / norm_now * direction
                norm_now = norm_next
    return (estimate, weights.reshape(1, pair_count, slot_count))


def solution(mesh):
    return jax.shard_map(
        on_device,
        mesh=mesh,
        in_specs=(
            P(None, "blk", None, "rep"),
            P(None, "blk", None, "rep"),
            P(None, "blk", None, "rep"),
            P("blk", None, "rep"),
            P("blk", None, "rep"),
            P("blk", None, "rep"),
            P(None, "blk"),
            P("blk"),
        ),
        out_specs=(P(None, "blk"), P("blk", None, "rep")),
        check_vma=False,
    )
```

profile of v0, /device:TPU:0, one launch (start us, length us, event | category | flops | bytes accessed | tf_op | source)
XLA Modules:
  0.0 1505.5 jit_solution(13354158175996071067)
XLA Ops:
  16.6 17.3 %gather_fusion.1 = f32[6144,3]{1,0:T(8,128)S(1)} fusion(f32[3,2048]{0,1:T(8,128)} %copy.781, s32[6144]{0:T(1024)S(1)} %broadcast_clamp_fusion), kind=kCustom, calls=%fused_computation.1 | custom fusion | bytes 172032 | tf_op jit(solution)/shard_map/gather | solution.py:146
  64.2 24.3 %gather_fusion = f32[6144,3]{1,0:T(8,128)} fusion(f32[3,16384]{0,1:T(8,128)} %copy.780, s32[6144]{0:T(1024)S(1)} %broadcast_clamp_fusion.1), kind=kCustom, calls=%fused_computation | custom fusion | bytes 172032 | tf_op jit(solution)/shard_map/gather | solution.py:146
  132.0 37.4 %scatter_custom_fusion = f32[9,16384]{0,1:T(8,128)} fusion(s32[6144]{0:T(1024)} %bitcast.235, f32[6144,9]{1,0:T(8,128)} %copy.791, f32[]{:T(128)} %constant.7.clone.1), kind=kCustom, calls=%fused_computation.39 | custom fusion | flops 55296 | bytes 590336 | tf_op jit(solution)/shard_map/vmap()/scatter-add | solution.py:85
  213.9 32.3 %scatter_fusion = f32[9,2048]{0,1:T(8,128)} fusion(f32[9,2048]{0,1:T(8,128)} %bitcast.191, s32[6144]{0:T(1024)S(1)} %reshape.813, f32[6144,9]{1,0:T(8,128)} %copy.799), kind=kCustom, calls=%fused_computation.13 | custom fusion | flops 55296 | bytes 688128 | tf_op jit(solution)/shard_map/vmap()/scatter-add | solution.py:85
  251.1 20.2 %all-reduce.5.cloned.1.call-done = f32[9,2048]{1,0:T(8,128)} async-done(((f32[9,2048]{1,0:T(8,128)}), f32[9,2048]{1,0:T(8,128)}) %all-reduce.5.cloned.1.call-update) | async-done | bytes 73744 | tf_op jit(solution)/shard_map/psum | solution.py:131
  283.4 22.1 %gather_fusion.3 = f32[6144,3]{1,0:T(8,128)} fusion(f32[3,2048]{0,1:T(8,128)} %copy.802, s32[6144]{0:T(1024)S(1)} %broadcast_clamp_fusion), kind=kCustom, calls=%fused_computation.3 | custom fusion | bytes 172032 | tf_op jit(solution)/shard_map/gather | solution.py:161
  323.0 24.3 %gather_fusion.2 = f32[6144,3]{1,0:T(8,128)} fusion(f32[3,16384]{0,1:T(8,128)} %copy.801, s32[6144]{0:T(1024)S(1)} %broadcast_clamp_fusion.1), kind=kCustom, calls=%fused_computation.2 | custom fusion | bytes 172032 | tf_op jit(solution)/shard_map/gather | solution.py:161
  352.2 34.2 %scatter_custom_fusion.2 = f32[3,16384]{0,1:T(8,128)} fusion(s32[6144]{0:T(1024)} %bitcast.236, f32[]{:T(128)} %constant.7.clone.1, f32[3,6144]{0,1:T(8,128)} %fusion.21), kind=kCustom, calls=%fused_computation.35 | custom fusion | flops 18432 | bytes 3342848 | tf_op jit(solution)/shard_map/vmap()/scatter-add | solution.py:85
  424.2 32.3 %scatter_fusion.1 = f32[3,2048]{0,1:T(8,128)} fusion(f32[3,2048]{0,1:T(8,128)} %bitcast.194, s32[6144]{0:T(1024)S(1)} %reshape.813, f32[6144,3]{1,0:T(8,128)} %copy.809), kind=kCustom, calls=%fused_computation.15 | custom fusion | flops 18432 | bytes 245760 | tf_op jit(solution)/shard_map/vmap()/scatter-add | solution.py:85
  468.7 30.2 %all-reduce.1 = (f32[]{:T(128)}, f32[]{:T(128)}) all-reduce(f32[]{:T(128)} %get-tuple-element.31, f32[]{:T(128)} %get-tuple-element.30), channel_id=1, replica_groups=mesh['blk'=16,'rep'=2] {'blk'}, use_global_device_ids=true, to_apply=%region_13.0 | all-reduce | flops 2 | bytes 16 | tf_op jit(solution)/shard_map/psum | solution.py:140
  504.2 30.1 %psum.102 = f32[]{:T(128)} all-reduce(f32[]{:T(128)} %multiply_reduce_fusion.17), channel_id=1, replica_groups=mesh['blk'=16,'rep'=2] {'blk'}, use_global_device_ids=true, to_apply=%region_22.0 | all-reduce | flops 1 | bytes 8 | tf_op jit(solution)/shard_map/psum | solution.py:140
  540.8 22.1 %gather_fusion.5 = f32[6144,3]{1,0:T(8,128)} fusion(f32[3,2048]{0,1:T(8,128)} %copy.811, s32[6144]{0:T(1024)S(1)} %broadcast_clamp_fusion), kind=kCustom, calls=%fused_computation.5 | custom fusion | bytes 172032 | tf_op jit(solution)/shard_map/gather | solution.py:161
  588.8 24.3 %gather_fusion.4 = f32[6144,3]{1,0:T(8,128)} fusion(f32[3,16384]{0,1:T(8,128)} %pad_maximum_fusion, s32[6144]{0:T(1024)S(1)} %broadcast_clamp_fusion.1), kind=kCustom, calls=%fused_computation.4 | custom fusion | bytes 172032 | tf_op jit(solution)/shard_map/gather | solution.py:161
  618.1 34.2 %scatter_custom_fusion.4 = f32[3,16384]{0,1:T(8,128)} fusion(s32[6144]{0:T(1024)} %bitcast.237, f32[]{:T(128)} %constant.7.clone.1, f32[3,6144]{0,1:T(8,128)} %fusion.19), kind=kCustom, calls=%fused_computation.33 | custom fusion | flops 18432 | bytes 3342848 | tf_op jit(solution)/shard_map/vmap()/scatter-add | solution.py:85
  685.2 33.9 %scatter_fusion.2 = f32[3,2048]{0,1:T(8,128)S(1)} fusion(f32[3,2048]{0,1:T(8,128)S(1)} %bitcast.195, s32[6144]{0:T(1024)S(1)} %reshape.813, f32[6144,3]{1,0:T(8,128)} %copy.822), kind=kCustom, calls=%fused_computation.17 | custom fusion | flops 18432 | bytes 245760 | tf_op jit(solution)/shard_map/vmap()/scatter-add | solution.py:85
  728.5 30.3 %psum.104 = f32[]{:T(128)} all-reduce(f32[]{:T(128)} %multiply_reduce_fusion.16), channel_id=1, replica_groups=mesh['blk'=16,'rep'=2] {'blk'}, use_global_device_ids=true, to_apply=%region_29.0 | all-reduce | flops 1 | bytes 8 | tf_op jit(solution)/shard_map/psum | solution.py:164
  762.2 20.9 %gather_fusion.7 = f32[6144,3]{1,0:T(8,128)} fusion(f32[3,2048]{0,1:T(8,128)S(1)} %copy.824, s32[6144]{0:T(1024)S(1)} %broadcast_clamp_fusion), kind=kCustom, calls=%fused_computation.7 | custom fusion | bytes 172032 | tf_op jit(solution)/shard_map/gather | solution.py:146
  804.7 24.3 %gather_fusion.6 = f32[6144,3]{1,0:T(8,128)} fusion(f32[3,16384]{0,1:T(8,128)} %pad_maximum_fusion.1, s32[6144]{0:T(1024)S(1)} %broadcast_clamp_fusion.1), kind=kCustom, calls=%fused_computation.6 | custom fusion | bytes 172032 | tf_op jit(solution)/shard_map/gather | solution.py:146
  872.6 37.2 %scatter_custom_fusion.6 = f32[9,16384]{0,1:T(8,128)} fusion(s32[6144]{0:T(1024)} %bitcast.238, f32[6144,9]{1,0:T(8,128)} %copy.836, f32[]{:T(128)} %constant.7.clone.1), kind=kCustom, calls=%fused_computation.37 | custom fusion | flops 55296 | bytes 590336 | tf_op jit(solution)/shard_map/vmap()/scatter-add | solution.py:85
  953.1 32.3 %scatter_fusion.3 = f32[9,2048]{0,1:T(8,128)} fusion(f32[9,2048]{0,1:T(8,128)} %bitcast.192, s32[6144]{0:T(1024)S(1)} %reshape.813, f32[6144,9]{1,0:T(8,128)} %copy.841), kind=kCustom, calls=%fused_computation.19 | custom fusion | flops 55296 | bytes 688128 | tf_op jit(solution)/shard_map/vmap()/scatter-add | solution.py:85
  987.7 20.7 %all-reduce.7.cloned.1.call-done = f32[9,2048]{1,0:T(8,128)} async-done(((f32[9,2048]{1,0:T(8,128)}), f32[9,2048]{1,0:T(8,128)}) %all-reduce.7.cloned.1.call-update) | async-done | bytes 73744 | tf_op jit(solution)/shard_map/psum | solution.py:131
  1020.4 22.1 %gather_fusion.9 = f32[6144,3]{1,0:T(8,128)} fusion(f32[3,2048]{0,1:T(8,128)} %copy.844, s32[6144]{0:T(1024)S(1)} %broadcast_clamp_fusion), kind=kCustom, calls=%fused_computation.9 | custom fusion | bytes 172032 | tf_op jit(solution)/shard_map/gather | solution.py:161
  1059.8 24.3 %gather_fusion.8 = f32[6144,3]{1,0:T(8,128)} fusion(f32[3,16384]{0,1:T(8,128)} %copy.843, s32[6144]{0:T(1024)S(1)} %broadcast_clamp_fusion.1), kind=kCustom, calls=%fused_computation.8 | custom fusion | bytes 172032 | tf_op jit(solution)/shard_map/gather | solution.py:161
  1089.0 34.2 %scatter_custom_fusion.8 = f32[3,16384]{0,1:T(8,128)} fusion(s32[6144]{0:T(1024)} %bitcast.239, f32[]{:T(128)} %constant.7.clone.1, f32[3,6144]{0,1:T(8,128)} %fusion.17), kind=kCustom, calls=%fused_computation.31 | custom fusion | flops 18432 | bytes 3342848 | tf_op jit(solution)/shard_map/vmap()/scatter-add | solution.py:85
  1160.9 32.3 %scatter_fusion.4 = f32[3,2048]{0,1:T(8,128)} fusion(f32[3,2048]{0,1:T(8,128)} %bitcast.196, s32[6144]{0:T(1024)S(1)} %reshape.813, f32[6144,3]{1,0:T(8,128)} %copy.851), kind=kCustom, calls=%fused_computation.21 | custom fusion | flops 18432 | bytes 245760 | tf_op jit(solution)/shard_map/vmap()/scatter-add | solution.py:85
  1205.4 30.2 %all-reduce = (f32[]{:T(128)}, f32[]{:T(128)}) all-reduce(f32[]{:T(128)} %get-tuple-element.29, f32[]{:T(128)} %get-tuple-element.28), channel_id=1, replica_groups=mesh['blk'=16,'rep'=2] {'blk'}, use_global_device_ids=true, to_apply=%region_43.0 | all-reduce | flops 2 | bytes 16 | tf_op jit(solution)/shard_map/psum | solution.py:140
  1241.0 30.2 %psum.109 = f32[]{:T(128)} all-reduce(f32[]{:T(128)} %multiply_reduce_fusion.13), channel_id=1, replica_groups=mesh['blk'=16,'rep'=2] {'blk'}, use_global_device_ids=true, to_apply=%region_52.0 | all-reduce | flops 1 | bytes 8 | tf_op jit(solution)/shard_map/psum | solution.py:140
  1277.9 22.1 %gather_fusion.11 = f32[6144,3]{1,0:T(8,128)} fusion(f32[3,2048]{0,1:T(8,128)} %copy.853, s32[6144]{0:T(1024)S(1)} %broadcast_clamp_fusion), kind=kCustom, calls=%fused_computation.11 | custom fusion | bytes 172032 | tf_op jit(solution)/shard_map/gather | solution.py:161
  1326.0 24.3 %gather_fusion.10 = f32[6144,3]{1,0:T(8,128)} fusion(f32[3,16384]{0,1:T(8,128)} %pad_maximum_fusion.2, s32[6144]{0:T(1024)S(1)} %broadcast_clamp_fusion.1), kind=kCustom, calls=%fused_computation.10 | custom fusion | bytes 172032 | tf_op jit(solution)/shard_map/gather | solution.py:161
  1355.2 34.2 %scatter_custom_fusion.10 = f32[3,16384]{0,1:T(8,128)} fusion(s32[6144]{0:T(1024)} %bitcast.240, f32[]{:T(128)} %constant.7.clone.1, f32[3,6144]{0,1:T(8,128)} %fusion.15), kind=kCustom, calls=%fused_computation.29 | custom fusion | flops 18432 | bytes 3342848 | tf_op jit(solution)/shard_map/vmap()/scatter-add | solution.py:85
  1422.3 33.9 %scatter_fusion.5 = f32[3,2048]{0,1:T(8,128)S(1)} fusion(f32[3,2048]{0,1:T(8,128)S(1)} %bitcast.193, s32[6144]{0:T(1024)S(1)} %reshape.813, f32[6144,3]{1,0:T(8,128)} %copy.864), kind=kCustom, calls=%fused_computation.23 | custom fusion | flops 18432 | bytes 245760 | tf_op jit(solution)/shard_map/vmap()/scatter-add | solution.py:85
  1466.3 30.1 %psum.111 = f32[]{:T(128)} all-reduce(f32[]{:T(128)} %multiply_reduce_fusion.12), channel_id=1, replica_groups=mesh['blk'=16,'rep'=2] {'blk'}, use_global_device_ids=true, to_apply=%region_59.0 | all-reduce | flops 1 | bytes 8 | tf_op jit(solution)/shard_map/psum | solution.py:164
  (456 shorter events, 579.4 us)
Async XLA Ops:
  7.2 264.2 %all-reduce.5.cloned.1.call-start = ((), (), s32[]{:S(2)}) async-start(), calls=%async_computation | async-start | bytes 262144 | tf_op jit(solution)/shard_map/psum | solution.py:131
  7.2 31.1 %collective-permute-start = (f32[3,2048]{1,0:T(4,128)}, f32[3,2048]{1,0:T(4,128)}, u32[]{:S(2)}, u32[]{:S(2)}) collective-permute-start(f32[3,2048]{1,0:T(4,128)} %param.14), channel_id=1, source_target_pairs={{0,30},{2,0},{4,2},{6,4},{8,6},{10,8},{12,10},{14,12},{16,14},{18,... | collective-permute-start | bytes 73736 | tf_op jit(solution)/shard_map/ppermute | solution.py:16
  44.2 14.1 collective-permute-start.2
  180.2 9.3 collective-permute-start.3
  191.4 8.2 collective-permute-start.4
  202.0 8.0 collective-permute-start.5
  248.5 759.9 %all-reduce.7.cloned.1.call-start = ((), (), s32[]{:S(2)}) async-start(), calls=%async_computation.1 | async-start | bytes 262144 | tf_op jit(solution)/shard_map/psum | solution.py:131
  280.2 28.3 %collective-permute-start.7 = (f32[3,4096]{1,0:T(4,128)}, f32[3,4096]{1,0:T(4,128)}, u32[]{:S(2)}, u32[]{:S(2)}) collective-permute-start(f32[3,4096]{1,0:T(4,128)} %pad_maximum_fusion.14), channel_id=1, source_target_pairs={{0,28},{2,30},{4,0},{6,2},{8,4},{10,6},{12,8},{14,10},{16,12},{18,... | collective-permute-start | bytes 147464 | tf_op jit(solution)/shard_map/ppermute | solution.py:16
  310.0 5.7 collective-permute-start.8
  397.3 7.9 collective-permute-start.9
  406.2 6.8 collective-permute-start.10
  414.3 6.3 collective-permute-start.11
  538.6 27.2 %collective-permute-start.13 = (f32[3,4096]{1,0:T(4,128)}, f32[3,4096]{1,0:T(4,128)}, u32[]{:S(2)}, u32[]{:S(2)}) collective-permute-start(f32[3,4096]{1,0:T(4,128)} %pad_maximum_fusion.15), channel_id=1, source_target_pairs={{0,28},{2,30},{4,0},{6,2},{8,4},{10,6},{12,8},{14,10},{16,12},{18,... | collective-permute-start | bytes 147464 | tf_op jit(solution)/shard_map/ppermute | solution.py:16
  567.4 9.9 collective-permute-start.14
  663.3 7.6 collective-permute-start.15
  671.9 6.8 collective-permute-start.16
  678.8 6.0 collective-permute-start.17
  761.8 23.7 %collective-permute-start.19 = (f32[3,4096]{1,0:T(4,128)S(1)}, f32[3,4096]{1,0:T(4,128)S(1)}, u32[]{:S(2)}, u32[]{:S(2)}) collective-permute-start(f32[3,4096]{1,0:T(4,128)S(1)} %pad_maximum_fusion.16), channel_id=1, source_target_pairs={{0,28},{2,30},{4,0},{6,2},{8,4},{10,6},{12,8},{14,10},{16,12},{18,... | collective-permute-start | bytes 147464 | tf_op jit(solution)/shard_map/ppermute | solution.py:16
  786.2 6.2 collective-permute-start.20
  920.7 9.3 collective-permute-start.21
  931.2 8.0 collective-permute-start.22
  940.7 8.5 collective-permute-start.23
  1017.2 28.3 %collective-permute-start.25 = (f32[3,4096]{1,0:T(4,128)}, f32[3,4096]{1,0:T(4,128)}, u32[]{:S(2)}, u32[]{:S(2)}) collective-permute-start(f32[3,4096]{1,0:T(4,128)} %pad_maximum_fusion.17), channel_id=1, source_target_pairs={{0,28},{2,30},{4,0},{6,2},{8,4},{10,6},{12,8},{14,10},{16,12},{18,... | collective-permute-start | bytes 147464 | tf_op jit(solution)/shard_map/ppermute | solution.py:16
  1047.0 5.4 collective-permute-start.26
  1134.0 7.9 collective-permute-start.27
  1143.0 6.8 collective-permute-start.28
  1151.1 6.3 collective-permute-start.29
  1275.8 27.2 %collective-permute-start.31 = (f32[3,4096]{1,0:T(4,128)}, f32[3,4096]{1,0:T(4,128)}, u32[]{:S(2)}, u32[]{:S(2)}) collective-permute-start(f32[3,4096]{1,0:T(4,128)} %pad_maximum_fusion.18), channel_id=1, source_target_pairs={{0,28},{2,30},{4,0},{6,2},{8,4},{10,6},{12,8},{14,10},{16,12},{18,... | collective-permute-start | bytes 147464 | tf_op jit(solution)/shard_map/ppermute | solution.py:16
  1304.5 9.9 collective-permute-start.32
  1400.4 7.6 collective-permute-start.33
  1409.0 6.8 collective-permute-start.34
  1415.9 6.0 collective-permute-start.35
  (80 other events, 1083.4 us)
Sparse Core Ops, SparseCore 0:
  248.6 22.7 all-reduce.4
  987.8 20.5 all-reduce.6
where the time goes:
time: 1510 us
  local copies, waits for them, and re-layouts  571 us (38%)
  other arithmetic  551 us (36%)
  blocking collectives  215 us (14%)
  waiting for transfers between devices  93.6 us (6%)
  starting transfers between devices  51.1 us (3%)
  between operations  23.4 us (2%)
    scatter-add x12, other arithmetic, spread(): jax.ops.segment_sum(values, index, num_segments=total)  408 us
    gather x12, local copies, waits for them, and re-layouts, on_device(): changed = window[:, second] - rotate(rotation, direction[:, first])  197 us
    psum x4, blocking collectives, precond_sum(): return lax.psum(jnp.sum(residual * scaled), 'blk')  121 us
    unnamed x174, local copies, waits for them, and re-layouts  61.6 us
    psum x2, blocking collectives, on_device(): step_size = norm_now / lax.psum(jnp.sum(direction * image), 'blk')  60.4 us
    ppermute x36, waiting for transfers between devices, shifted(): return lax.ppermute(value, axis, pairs)  52.6 us
    ppermute x36, starting transfers between devices, shifted(): return lax.ppermute(value, axis, pairs)  51 us
    gather x2, local copies, waits for them, and re-layouts, on_device(): window[:, second] - rotate(rotation, estimate[:, first])  48.6 us
  transfers between devices with their start and end apart: 38, of which 21 were waited for; matrix products, arithmetic and copies ran while one was open for 18% of the time, Pallas kernels for 0%

commit v1 on v0

--- a/solution.py
+++ b/solution.py
@@ -128,7 +128,7 @@
         return current[:, 0]
 
     def reduce_halves(sums):
-        return lax.psum(sums, "rep")
+        return jnp.sum(lax.all_gather(sums, "rep"), axis=0)
 
     def collect(far_terms, near_terms):
         channels = far_terms.shape[0]

time: 1510 us -> 1460 us (0.967)
  waiting for transfers between devices: 93.6 us -> 46.7 us
    psum x2 -> x0, waiting for transfers between devices: 40.9 us -> none  [reduce_halves(): return lax.psum(sums, 'rep')]
    psum x4 -> x0, blocking collectives: 33.9 us -> none  [reduce_halves(): return lax.psum(sums, 'rep')]
    all_gather x0 -> x6, blocking collectives: none -> 33.6 us  [reduce_halves(): return jnp.sum(lax.all_gather(sums, 'rep'), axis=0)]
    unnamed x174 -> x180, local copies, waits for them, and re-layouts: 61.6 us -> 70.9 us
  transfers between devices with their start and end apart: 38 -> 36, of which waited for: 21 -> 19; matrix products, arithmetic and copies ran while one was open for 18% -> 18% of each run, Pallas kernels for 0% -> 0%
where the time goes in v1:
time: 1460 us; the launch traced here: 1450 us
  local copies, waits for them, and re-layouts  571 us (39%)
  other arithmetic  558 us (38%)
  blocking collectives  216 us (15%)
  starting transfers between devices  51.9 us (4%)
  waiting for transfers between devices  46.7 us (3%)
    scatter-add x12, other arithmetic, spread(): jax.ops.segment_sum(values, index, num_segments=total)  408 us
    gather x12, local copies, waits for them, and re-layouts, on_device(): changed = window[:, second] - rotate(rotation, direction[:, first])  197 us
    psum x4, blocking collectives, precond_sum(): return lax.psum(jnp.sum(residual * scaled), 'blk')  122 us
    unnamed x180, local copies, waits for them, and re-layouts  70.9 us
    psum x2, blocking collectives, on_device(): step_size = norm_now / lax.psum(jnp.sum(direction * image), 'blk')  60.2 us
    ppermute x36, starting transfers between devices, shifted(): return lax.ppermute(value, axis, pairs)  51.9 us
    gather x2, local copies, waits for them, and re-layouts, on_device(): window[:, second] - rotate(rotation, estimate[:, first])  48.6 us
    slice x18, local copies, waits for them, and re-layouts, returned(): moved = shifted(current[:, half_width:width], 'blk', half_width)  47.8 us
  transfers between devices with their start and end apart: 36, of which 19 were waited for; matrix products, arithmetic and copies ran while one was open for 18% of the time, Pallas kernels for 0%

profile of v1, /device:TPU:0, one launch (start us, length us, event | category | flops | bytes accessed | tf_op | source)
XLA Modules:
  0.0 1453.1 jit_solution(4037688807136227678)
XLA Ops:
  10.0 17.3 %gather_fusion.1 = f32[6144,3]{1,0:T(8,128)S(1)} fusion(f32[3,2048]{0,1:T(8,128)} %copy.819, s32[6144]{0:T(1024)S(1)} %broadcast_clamp_fusion), kind=kCustom, calls=%fused_computation.1 | custom fusion | bytes 172032 | tf_op jit(solution)/shard_map/gather | solution.py:146
  57.6 24.3 %gather_fusion = f32[6144,3]{1,0:T(8,128)} fusion(f32[3,16384]{0,1:T(8,128)} %copy.818, s32[6144]{0:T(1024)S(1)} %broadcast_clamp_fusion.1), kind=kCustom, calls=%fused_computation | custom fusion | bytes 172032 | tf_op jit(solution)/shard_map/gather | solution.py:146
  89.3 9.5 fusion.12
  125.4 37.4 %scatter_custom_fusion = f32[9,16384]{0,1:T(8,128)} fusion(s32[6144]{0:T(1024)} %bitcast.247, f32[6144,9]{1,0:T(8,128)} %copy.829, f32[]{:T(128)} %constant.7.clone.1), kind=kCustom, calls=%fused_computation.39 | custom fusion | flops 55296 | bytes 590336 | tf_op jit(solution)/shard_map/vmap()/scatter-add | solution.py:85
  207.4 32.3 %scatter_fusion = f32[9,2048]{0,1:T(8,128)} fusion(f32[9,2048]{0,1:T(8,128)} %bitcast.197, s32[6144]{0:T(1024)S(1)} %reshape.813, f32[6144,9]{1,0:T(8,128)} %copy.837), kind=kCustom, calls=%fused_computation.13 | custom fusion | flops 55296 | bytes 688128 | tf_op jit(solution)/shard_map/vmap()/scatter-add | solution.py:85
  261.8 22.1 %gather_fusion.3 = f32[6144,3]{1,0:T(8,128)} fusion(f32[3,2048]{0,1:T(8,128)} %copy.840, s32[6144]{0:T(1024)S(1)} %broadcast_clamp_fusion), kind=kCustom, calls=%fused_computation.3 | custom fusion | bytes 172032 | tf_op jit(solution)/shard_map/gather | solution.py:161
  301.0 24.3 %gather_fusion.2 = f32[6144,3]{1,0:T(8,128)} fusion(f32[3,16384]{0,1:T(8,128)} %copy.839, s32[6144]{0:T(1024)S(1)} %broadcast_clamp_fusion.1), kind=kCustom, calls=%fused_computation.2 | custom fusion | bytes 172032 | tf_op jit(solution)/shard_map/gather | solution.py:161
  330.3 34.2 %scatter_custom_fusion.2 = f32[3,16384]{0,1:T(8,128)} fusion(s32[6144]{0:T(1024)} %bitcast.248, f32[]{:T(128)} %constant.7.clone.1, f32[3,6144]{0,1:T(8,128)} %fusion.21), kind=kCustom, calls=%fused_computation.35 | custom fusion | flops 18432 | bytes 3342848 | tf_op jit(solution)/shard_map/vmap()/scatter-add | solution.py:85
  402.8 32.3 %scatter_fusion.1 = f32[3,2048]{0,1:T(8,128)} fusion(f32[3,2048]{0,1:T(8,128)} %bitcast.203, s32[6144]{0:T(1024)S(1)} %reshape.813, f32[6144,3]{1,0:T(8,128)} %copy.847), kind=kCustom, calls=%fused_computation.15 | custom fusion | flops 18432 | bytes 245760 | tf_op jit(solution)/shard_map/vmap()/scatter-add | solution.py:85
  445.1 30.7 %all-reduce.1 = (f32[]{:T(128)}, f32[]{:T(128)}) all-reduce(f32[]{:T(128)} %get-tuple-element.31, f32[]{:T(128)} %get-tuple-element.30), channel_id=1, replica_groups=mesh['blk'=16,'rep'=2] {'blk'}, use_global_device_ids=true, to_apply=%region_13.0 | all-reduce | flops 2 | bytes 16 | tf_op jit(solution)/shard_map/psum | solution.py:140
  481.0 30.1 %psum.58 = f32[]{:T(128)} all-reduce(f32[]{:T(128)} %multiply_reduce_fusion.17), channel_id=1, replica_groups=mesh['blk'=16,'rep'=2] {'blk'}, use_global_device_ids=true, to_apply=%region_22.0 | all-reduce | flops 1 | bytes 8 | tf_op jit(solution)/shard_map/psum | solution.py:140
  517.6 22.1 %gather_fusion.5 = f32[6144,3]{1,0:T(8,128)} fusion(f32[3,2048]{0,1:T(8,128)} %copy.849, s32[6144]{0:T(1024)S(1)} %broadcast_clamp_fusion), kind=kCustom, calls=%fused_computation.5 | custom fusion | bytes 172032 | tf_op jit(solution)/shard_map/gather | solution.py:161
  565.7 24.3 %gather_fusion.4 = f32[6144,3]{1,0:T(8,128)} fusion(f32[3,16384]{0,1:T(8,128)} %pad_maximum_fusion, s32[6144]{0:T(1024)S(1)} %broadcast_clamp_fusion.1), kind=kCustom, calls=%fused_computation.4 | custom fusion | bytes 172032 | tf_op jit(solution)/shard_map/gather | solution.py:161
  595.0 34.2 %scatter_custom_fusion.4 = f32[3,16384]{0,1:T(8,128)} fusion(s32[6144]{0:T(1024)} %bitcast.249, f32[]{:T(128)} %constant.7.clone.1, f32[3,6144]{0,1:T(8,128)} %fusion.19), kind=kCustom, calls=%fused_computation.33 | custom fusion | flops 18432 | bytes 3342848 | tf_op jit(solution)/shard_map/vmap()/scatter-add | solution.py:85
  662.1 33.9 %scatter_fusion.2 = f32[3,2048]{0,1:T(8,128)S(1)} fusion(f32[3,2048]{0,1:T(8,128)S(1)} %bitcast.205, s32[6144]{0:T(1024)S(1)} %reshape.813, f32[6144,3]{1,0:T(8,128)} %copy.860), kind=kCustom, calls=%fused_computation.17 | custom fusion | flops 18432 | bytes 245760 | tf_op jit(solution)/shard_map/vmap()/scatter-add | solution.py:85
  701.6 30.1 %psum.59 = f32[]{:T(128)} all-reduce(f32[]{:T(128)} %multiply_reduce_fusion.16), channel_id=1, replica_groups=mesh['blk'=16,'rep'=2] {'blk'}, use_global_device_ids=true, to_apply=%region_29.0 | all-reduce | flops 1 | bytes 8 | tf_op jit(solution)/shard_map/psum | solution.py:164
  735.4 20.9 %gather_fusion.7 = f32[6144,3]{1,0:T(8,128)} fusion(f32[3,2048]{0,1:T(8,128)S(1)} %copy.862, s32[6144]{0:T(1024)S(1)} %broadcast_clamp_fusion), kind=kCustom, calls=%fused_computation.7 | custom fusion | bytes 172032 | tf_op jit(solution)/shard_map/gather | solution.py:146
  777.9 24.3 %gather_fusion.6 = f32[6144,3]{1,0:T(8,128)} fusion(f32[3,16384]{0,1:T(8,128)} %pad_maximum_fusion.1, s32[6144]{0:T(1024)S(1)} %broadcast_clamp_fusion.1), kind=kCustom, calls=%fused_computation.6 | custom fusion | bytes 172032 | tf_op jit(solution)/shard_map/gather | solution.py:146
  810.2 9.7 fusion.13
  845.8 37.2 %scatter_custom_fusion.6 = f32[9,16384]{0,1:T(8,128)} fusion(s32[6144]{0:T(1024)} %bitcast.250, f32[6144,9]{1,0:T(8,128)} %copy.874, f32[]{:T(128)} %constant.7.clone.1), kind=kCustom, calls=%fused_computation.37 | custom fusion | flops 55296 | bytes 590336 | tf_op jit(solution)/shard_map/vmap()/scatter-add | solution.py:85
  926.3 32.3 %scatter_fusion.3 = f32[9,2048]{0,1:T(8,128)} fusion(f32[9,2048]{0,1:T(8,128)} %bitcast.199, s32[6144]{0:T(1024)S(1)} %reshape.813, f32[6144,9]{1,0:T(8,128)} %copy.879), kind=kCustom, calls=%fused_computation.19 | custom fusion | flops 55296 | bytes 688128 | tf_op jit(solution)/shard_map/vmap()/scatter-add | solution.py:85
  979.5 22.1 %gather_fusion.9 = f32[6144,3]{1,0:T(8,128)} fusion(f32[3,2048]{0,1:T(8,128)} %copy.882, s32[6144]{0:T(1024)S(1)} %broadcast_clamp_fusion), kind=kCustom, calls=%fused_computation.9 | custom fusion | bytes 172032 | tf_op jit(solution)/shard_map/gather | solution.py:161
  1019.5 24.3 %gather_fusion.8 = f32[6144,3]{1,0:T(8,128)} fusion(f32[3,16384]{0,1:T(8,128)} %copy.881, s32[6144]{0:T(1024)S(1)} %broadcast_clamp_fusion.1), kind=kCustom, calls=%fused_computation.8 | custom fusion | bytes 172032 | tf_op jit(solution)/shard_map/gather | solution.py:161
  1048.8 34.2 %scatter_custom_fusion.8 = f32[3,16384]{0,1:T(8,128)} fusion(s32[6144]{0:T(1024)} %bitcast.251, f32[]{:T(128)} %constant.7.clone.1, f32[3,6144]{0,1:T(8,128)} %fusion.17), kind=kCustom, calls=%fused_computation.31 | custom fusion | flops 18432 | bytes 3342848 | tf_op jit(solution)/shard_map/vmap()/scatter-add | solution.py:85
  1120.5 32.3 %scatter_fusion.4 = f32[3,2048]{0,1:T(8,128)} fusion(f32[3,2048]{0,1:T(8,128)} %bitcast.207, s32[6144]{0:T(1024)S(1)} %reshape.813, f32[6144,3]{1,0:T(8,128)} %copy.889), kind=kCustom, calls=%fused_computation.21 | custom fusion | flops 18432 | bytes 245760 | tf_op jit(solution)/shard_map/vmap()/scatter-add | solution.py:85
  1162.8 30.9 %all-reduce = (f32[]{:T(128)}, f32[]{:T(128)}) all-reduce(f32[]{:T(128)} %get-tuple-element.29, f32[]{:T(128)} %get-tuple-element.28), channel_id=1, replica_groups=mesh['blk'=16,'rep'=2] {'blk'}, use_global_device_ids=true, to_apply=%region_43.0 | all-reduce | flops 2 | bytes 16 | tf_op jit(solution)/shard_map/psum | solution.py:140
  1199.1 30.2 %psum.62 = f32[]{:T(128)} all-reduce(f32[]{:T(128)} %multiply_reduce_fusion.13), channel_id=1, replica_groups=mesh['blk'=16,'rep'=2] {'blk'}, use_global_device_ids=true, to_apply=%region_52.0 | all-reduce | flops 1 | bytes 8 | tf_op jit(solution)/shard_map/psum | solution.py:140
  1236.0 22.1 %gather_fusion.11 = f32[6144,3]{1,0:T(8,128)} fusion(f32[3,2048]{0,1:T(8,128)} %copy.891, s32[6144]{0:T(1024)S(1)} %broadcast_clamp_fusion), kind=kCustom, calls=%fused_computation.11 | custom fusion | bytes 172032 | tf_op jit(solution)/shard_map/gather | solution.py:161
  1284.1 24.3 %gather_fusion.10 = f32[6144,3]{1,0:T(8,128)} fusion(f32[3,16384]{0,1:T(8,128)} %pad_maximum_fusion.2, s32[6144]{0:T(1024)S(1)} %broadcast_clamp_fusion.1), kind=kCustom, calls=%fused_computation.10 | custom fusion | bytes 172032 | tf_op jit(solution)/shard_map/gather | solution.py:161
  1313.3 34.2 %scatter_custom_fusion.10 = f32[3,16384]{0,1:T(8,128)} fusion(s32[6144]{0:T(1024)} %bitcast.252, f32[]{:T(128)} %constant.7.clone.1, f32[3,6144]{0,1:T(8,128)} %fusion.15), kind=kCustom, calls=%fused_computation.29 | custom fusion | flops 18432 | bytes 3342848 | tf_op jit(solution)/shard_map/vmap()/scatter-add | solution.py:85
  1380.4 33.9 %scatter_fusion.5 = f32[3,2048]{0,1:T(8,128)S(1)} fusion(f32[3,2048]{0,1:T(8,128)S(1)} %bitcast.201, s32[6144]{0:T(1024)S(1)} %reshape.813, f32[6144,3]{1,0:T(8,128)} %copy.902), kind=kCustom, calls=%fused_computation.23 | custom fusion | flops 18432 | bytes 245760 | tf_op jit(solution)/shard_map/vmap()/scatter-add | solution.py:85
  1420.7 30.1 %psum.63 = f32[]{:T(128)} all-reduce(f32[]{:T(128)} %multiply_reduce_fusion.12), channel_id=1, replica_groups=mesh['blk'=16,'rep'=2] {'blk'}, use_global_device_ids=true, to_apply=%region_59.0 | all-reduce | flops 1 | bytes 8 | tf_op jit(solution)/shard_map/psum | solution.py:164
  (458 shorter events, 561.0 us)
Async XLA Ops:
  0.6 31.1 %collective-permute-start = (f32[3,2048]{1,0:T(4,128)}, f32[3,2048]{1,0:T(4,128)}, u32[]{:S(2)}, u32[]{:S(2)}) collective-permute-start(f32[3,2048]{1,0:T(4,128)} %param.14), channel_id=1, source_target_pairs={{0,30},{2,0},{4,2},{6,4},{8,6},{10,8},{12,10},{14,12},{16,14},{18,... | collective-permute-start | bytes 73736 | tf_op jit(solution)/shard_map/ppermute | solution.py:16
  32.6 4.3 collective-permute-start.1
  37.7 14.1 collective-permute-start.2
  173.7 9.3 collective-permute-start.3
  184.8 8.2 collective-permute-start.4
  195.5 8.0 collective-permute-start.5
  253.7 5.2 collective-permute-start.6
  259.6 27.3 %collective-permute-start.7 = (f32[3,4096]{1,0:T(4,128)}, f32[3,4096]{1,0:T(4,128)}, u32[]{:S(2)}, u32[]{:S(2)}) collective-permute-start(f32[3,4096]{1,0:T(4,128)} %pad_maximum_fusion.14), channel_id=1, source_target_pairs={{0,28},{2,30},{4,0},{6,2},{8,4},{10,6},{12,8},{14,10},{16,12},{18,... | collective-permute-start | bytes 147464 | tf_op jit(solution)/shard_map/ppermute | solution.py:16
  288.4 5.3 collective-permute-start.8
  375.3 8.3 collective-permute-start.9
  384.6 6.8 collective-permute-start.10
  392.8 6.5 collective-permute-start.11
  515.5 27.2 %collective-permute-start.13 = (f32[3,4096]{1,0:T(4,128)}, f32[3,4096]{1,0:T(4,128)}, u32[]{:S(2)}, u32[]{:S(2)}) collective-permute-start(f32[3,4096]{1,0:T(4,128)} %pad_maximum_fusion.15), channel_id=1, source_target_pairs={{0,28},{2,30},{4,0},{6,2},{8,4},{10,6},{12,8},{14,10},{16,12},{18,... | collective-permute-start | bytes 147464 | tf_op jit(solution)/shard_map/ppermute | solution.py:16
  544.3 9.9 collective-permute-start.14
  640.2 7.6 collective-permute-start.15
  648.8 6.8 collective-permute-start.16
  655.7 6.0 collective-permute-start.17
  735.0 23.7 %collective-permute-start.19 = (f32[3,4096]{1,0:T(4,128)S(1)}, f32[3,4096]{1,0:T(4,128)S(1)}, u32[]{:S(2)}, u32[]{:S(2)}) collective-permute-start(f32[3,4096]{1,0:T(4,128)S(1)} %pad_maximum_fusion.16), channel_id=1, source_target_pairs={{0,28},{2,30},{4,0},{6,2},{8,4},{10,6},{12,8},{14,10},{16,12},{18,... | collective-permute-start | bytes 147464 | tf_op jit(solution)/shard_map/ppermute | solution.py:16
  759.4 6.2 collective-permute-start.20
  893.9 9.3 collective-permute-start.21
  904.4 8.0 collective-permute-start.22
  913.9 8.6 collective-permute-start.23
  977.3 27.3 %collective-permute-start.25 = (f32[3,4096]{1,0:T(4,128)}, f32[3,4096]{1,0:T(4,128)}, u32[]{:S(2)}, u32[]{:S(2)}) collective-permute-start(f32[3,4096]{1,0:T(4,128)} %pad_maximum_fusion.17), channel_id=1, source_target_pairs={{0,28},{2,30},{4,0},{6,2},{8,4},{10,6},{12,8},{14,10},{16,12},{18,... | collective-permute-start | bytes 147464 | tf_op jit(solution)/shard_map/ppermute | solution.py:16
  1006.1 6.1 collective-permute-start.26
  1093.8 7.8 collective-permute-start.27
  1102.6 6.8 collective-permute-start.28
  1110.7 6.3 collective-permute-start.29
  1233.9 27.2 %collective-permute-start.31 = (f32[3,4096]{1,0:T(4,128)}, f32[3,4096]{1,0:T(4,128)}, u32[]{:S(2)}, u32[]{:S(2)}) collective-permute-start(f32[3,4096]{1,0:T(4,128)} %pad_maximum_fusion.18), channel_id=1, source_target_pairs={{0,28},{2,30},{4,0},{6,2},{8,4},{10,6},{12,8},{14,10},{16,12},{18,... | collective-permute-start | bytes 147464 | tf_op jit(solution)/shard_map/ppermute | solution.py:16
  1262.6 9.9 collective-permute-start.32
  1358.5 7.6 collective-permute-start.33
  1367.1 6.8 collective-permute-start.34
  1374.0 6.0 collective-permute-start.35
  (78 other events, 982.4 us)
